TPU v7x, 32 devices: a whole 2x2x4 slice. The times are simulated.
32 devices in a mesh: seq: 4 (over y, x), seg: 4 (over z), head: 2 (over core).
Axes of the slice: x: 2, y: 2, z: 4, core: 2. Of those that a mesh axis runs over, the one named last changes fastest.
Arguments:
- queries: bfloat16 [8, 16384, 128], P('head', ('seg', 'seq')), may hold values from -6 to 6
- keys: bfloat16 [8, 16384, 128], P('head', ('seg', 'seq')), may hold values from -6 to 6
- values: bfloat16 [8, 16384, 128], P('head', ('seg', 'seq')), may hold values from -8 to 8
- teacher: bfloat16 [8, 16384, 128], P('head', ('seg', 'seq')), may hold values from -6 to 6
- query_proj: float32 [128, 16], replicated, may hold values from -0.5 to 0.5
- key_proj: float32 [128, 16], replicated, may hold values from -0.5 to 0.5
Outputs:
- student: bfloat16 [8, 16384, 128], P('head', ('seg', 'seq'))
- query_grad: float32 [128, 16], replicated
- key_grad: float32 [128, 16], replicated
All inputs are finite; a program needn't handle non-finite values.
Results may differ from a plain program's by a relative error of at most 0.0014.
The roundings to bfloat16 on the way count: a program that leaves them out, or rounds other values in their place, can miss the bound.
Values sent between devices are 32-bit elements; how exact they have to be, the bound alone decides.
No kernel may reach another device: no remote copies, remote signals or barrier semaphores. Data moves between devices by JAX's collectives and lax.ppermute only.
A program may use at most 64 MiB of HBM per device.

v0:
```python
import math
import jax
import jax.numpy as jnp
import numpy as np
from jax import lax
from jax.sharding import PartitionSpec as P

highest = lax.Precision.HIGHEST


def carried_in(value, axis, join, neutral, backward):
    count, mine = (lax.axis_size(axis), lax.axis_index(axis))
    pieces = jax.tree.map(lambda part: lax.all_gather(part, axis), value)
    if backward:
        pieces = jax.tree.map(lambda part: part[::-1], pieces)
        mine = count - 1 - mine
    running = jax.tree.map(
        lambda part, zero: jnp.full_like(part, 0) + jnp.asarray(zero, part.dtype), value, neutral
    )

    def step(position, running):
        longer = join(running, jax.tree.map(lambda part: part[position], pieces))
        return jax.tree.map(lambda new, old: jnp.where(position < mine, new, old), longer, running)

    return lax.fori_loop(0, count - 1, step, running)


def feature_tables(width):
    first, second = np.triu_indices(width)
    eye = np.eye(width)
    coef = np.where(first == second, 0.5**0.5, 1.0)
    return (
        jnp.asarray(eye[first], jnp.float32),
        jnp.asarray(eye[second], jnp.float32),
        jnp.asarray(coef, jnp.float32),
    )


def features(proj_t, tables):
    sel_a, sel_b, coef = tables
    left = jnp.dot(sel_a, proj_t, precision=highest)
    right = jnp.dot(sel_b, proj_t, precision=highest)
    return jnp.concatenate([jnp.ones_like(proj_t[:1]), proj_t, coef[:, None] * left * right], 0)


def feature_grad(proj_t, grad_phi, tables):
    sel_a, sel_b, coef = tables
    width = proj_t.shape[0]
    left = jnp.dot(sel_a, proj_t, precision=highest)
    right = jnp.dot(sel_b, proj_t, precision=highest)
    quad = grad_phi[1 + width :] * coef[:, None]
    return (
        grad_phi[1 : 1 + width]
        + jnp.dot(sel_a.T, quad * right, precision=highest)
        + jnp.dot(sel_b.T, quad * left, precision=highest)
    )


def project(weight_b, rows):
    return lax.dot_general(
        weight_b, rows, (((0,), (1,)), ((), ())), preferred_element_type=jnp.float32
    )


def head_state(q_h, k_h, v_h, wq_b, wk_b, tables):
    q_t = project(wq_b, q_h)
    k_t = project(wk_b, k_h)
    phi_k = features(k_t, tables)
    state = jnp.dot(phi_k.astype(jnp.bfloat16), v_h, preferred_element_type=jnp.float32)
    return (q_t, k_t, state, jnp.sum(phi_k, 1))


def head_forward(q_t, k_t, v_h, teacher_h, s_prev, z_prev, scale, tables):
    phi_q = features(q_t, tables)
    length = q_t.shape[1]
    scores = lax.dot_general(q_t, k_t, (((0,), (0,)), ((), ())), precision=highest)
    causal = jnp.arange(length)[:, None] >= jnp.arange(length)[None, :]
    weights = jnp.where(causal, 1.0 + scores + 0.5 * scores * scores, 0.0)
    numer = jnp.dot(weights.astype(jnp.bfloat16), v_h, preferred_element_type=jnp.float32)
    numer = numer + lax.dot_general(phi_q, s_prev, (((0,), (0,)), ((), ())), precision=highest)
    denom = jnp.sum(weights, 1) + jnp.dot(z_prev, phi_q, precision=highest)
    student = numer / denom[:, None]
    g_out = scale * (student - teacher_h.astype(jnp.float32))
    g_numer = g_out / denom[:, None]
    g_denom = -jnp.sum(g_out * student, 1) / denom
    g_weights = (
        lax.dot_general(
            g_numer.astype(jnp.bfloat16),
            v_h,
            (((1,), (1,)), ((), ())),
            preferred_element_type=jnp.float32,
        )
        + g_denom[:, None]
    )
    g_scores = jnp.where(causal, g_weights * (1.0 + scores), 0.0)
    g_q = lax.dot_general(k_t, g_scores, (((1,), (1,)), ((), ())), precision=highest)
    g_k = jnp.dot(q_t, g_scores, precision=highest)
    g_phi_q = (
        lax.dot_general(s_prev, g_numer, (((1,), (1,)), ((), ())), precision=highest)
        + z_prev[:, None] * g_denom[None, :]
    )
    g_q = g_q + feature_grad(q_t, g_phi_q, tables)
    g_state = jnp.dot(phi_q, g_numer, precision=highest)
    h_state = jnp.dot(phi_q, g_denom, precision=highest)
    return (student, g_q, g_k, g_state, h_state)


def head_grads(q_h, k_h, v_h, k_t, g_q, g_k, g_next, h_next, tables):
    g_phi_k = (
        lax.dot_general(
            g_next.astype(jnp.bfloat16),
            v_h,
            (((1,), (1,)), ((), ())),
            preferred_element_type=jnp.float32,
        )
        + h_next[:, None]
    )
    g_k = g_k + feature_grad(k_t, g_phi_k, tables)
    grad_q = lax.dot_general(
        q_h, g_q.astype(jnp.bfloat16), (((0,), (1,)), ((), ())), preferred_element_type=jnp.float32
    )
    grad_k = lax.dot_general(
        k_h, g_k.astype(jnp.bfloat16), (((0,), (1,)), ((), ())), preferred_element_type=jnp.float32
    )
    return (grad_q, grad_k)


def add_trees(first, second):
    return jax.tree.map(jnp.add, first, second)


def masked_fold(mine, backward, carry, piece):
    rows = piece[0].shape[0]
    index = jnp.arange(rows)
    keep = index > mine if backward else index < mine

    def pick(array):
        shaped = keep.reshape((rows,) + (1,) * (array.ndim - 1))
        return jnp.sum(jnp.where(shaped, array, 0.0), 0)

    part = jax.tree.map(pick, piece)
    whole = jax.tree.map(lambda array: jnp.sum(array, 0), piece)
    return (add_trees(carry[0], part), add_trees(carry[1], whole))


def carried(local, backward):
    zeros = jax.tree.map(jnp.zeros_like, local)
    stacked = jax.tree.map(lambda array: array[None], local)
    inner, totals = masked_fold(
        lax.axis_index("seq"),
        backward,
        (zeros, zeros),
        (
            lax.all_gather(stacked[0], "seq", axis=0, tiled=True),
            lax.all_gather(stacked[1], "seq", axis=0, tiled=True),
        ),
    )
    outer = carried_in(totals, "seg", add_trees, zeros, backward)
    return add_trees(inner, outer)


def shards(queries, keys, values, teacher, query_proj, key_proj):
    tables = feature_tables(query_proj.shape[1])
    wq_b = query_proj.astype(jnp.bfloat16)
    wk_b = key_proj.astype(jnp.bfloat16)
    q_t, k_t, states, counts = lax.map(
        lambda xs: head_state(xs[0], xs[1], xs[2], wq_b, wk_b, tables), (queries, keys, values)
    )
    s_prev, z_prev = carried((states, counts), False)
    heads_all = queries.shape[0] * lax.axis_size("head")
    tokens_all = queries.shape[1] * lax.axis_size("seq") * lax.axis_size("seg")
    scale = 1.0 / math.sqrt(heads_all * tokens_all)
    student, g_q, g_k, g_state, h_state = lax.map(
        lambda xs: head_forward(xs[0], xs[1], xs[2], xs[3], xs[4], xs[5], scale, tables),
        (q_t, k_t, values, teacher, s_prev, z_prev),
    )
    g_next, h_next = carried((g_state, h_state), True)
    grad_q, grad_k = lax.map(
        lambda xs: head_grads(xs[0], xs[1], xs[2], xs[3], xs[4], xs[5], xs[6], xs[7], tables),
        (queries, keys, values, k_t, g_q, g_k, g_next, h_next),
    )
    summed = lax.psum((jnp.sum(grad_q, 0), jnp.sum(grad_k, 0)), ("seq", "seg", "head"))
    return (student.astype(jnp.bfloat16), summed[0], summed[1])


def solution(mesh):
    in_specs = (
        P("head", ("seg", "seq"), None),
        P("head", ("seg", "seq"), None),
        P("head", ("seg", "seq"), None),
        P("head", ("seg", "seq"), None),
        P(),
        P(),
    )
    out_specs = (P("head", ("seg", "seq"), None), P(), P())
    return jax.shard_map(shards, mesh=mesh, in_specs=in_specs, out_specs=out_specs, check_vma=False)
```

profile of v0, /device:TPU:0, one launch (start us, length us, event | category | flops | bytes accessed | tf_op | source)
XLA Modules:
  0.0 344.7 jit_solution(8274270570329167139)
XLA Ops:
  8.7 27.1 %while.81 = (s32[]{:T(128)}, f32[4,16,1024]{2,1,0:T(8,128)S(1)}, f32[4,16,1024]{2,1,0:T(8,128)S(1)}, f32[4,153,128]{2,1,0:T(8,128)S(1)}, f32[4,153]{1,0:T(4,128)...) while((s32[]{:T(128)}, f32[4,16,1024]{2,1,0:T(8,128)S(1)}, ...), condition=%wide.region_2.3_spmd.clone, body=%wide.region_0.2_spmd.sunk.clone.sunk | while | flops 103662440 | bytes 4145861 | solution.py:166
  36.6 31.5 %all-gather.17.cloned.1.call-done = f32[16,153,128]{2,1,0:T(8,128)} async-done(((f32[4,153,128]{2,1,0:T(8,128)}), f32[16,153,128]{2,1,0:T(8,128)}) %all-gather.17.cloned.1.call-update) | async-done | bytes 1253392 | tf_op jit(solution)/shard_map/all_gather | solution.py:154
  68.1 2.4 fusion.90
  70.6 8.1 %all-gather.8 = f32[4,4,153]{2,1,0:T(4,128)S(1)} all-gather(f32[1,4,153]{2,1,0:T(4,128)S(1)} %bitcast.304), channel_id=4, replica_groups=mesh['seq'=4,'seg'=4,'head'=2] {'seq'}, dimensions={0}, use_global_device_ids=true | all-gather | bytes 12240 | tf_op jit(solution)/shard_map/all_gather | solution.py:155
  78.8 13.7 %all-gather.9 = f32[4,4,153]{2,1,0:T(4,128)S(1)} all-gather(f32[1,4,153]{2,1,0:T(4,128)S(1)} %bitcast.301), channel_id=5, replica_groups=mesh['seq'=4,'seg'=4,'head'=2] {'seg'}, dimensions={0}, use_global_device_ids=true | all-gather | bytes 12240 | tf_op jit(solution)/shard_map/all_gather | solution.py:13
  93.2 10.2 %all-gather.19.cloned.1.call-done = f32[16,153,128]{2,1,0:T(8,128)} async-done(((f32[4,153,128]{2,1,0:T(8,128)}), f32[16,153,128]{2,1,0:T(8,128)}) %all-gather.19.cloned.1.call-update) | async-done | bytes 1253392 | tf_op jit(solution)/shard_map/all_gather | solution.py:13
  103.4 3.4 while.84
  109.1 98.5 %while.82 = (s32[]{:T(128)}, bf16[4,1024,128]{2,1,0:T(8,128)(2,1)}, bf16[4,16,1024]{2,1,0:T(8,128)(2,1)}, f32[4,16,1024]{2,1,0:T(8,128)}, f32[4,153,128]{2,1,0:T...) while((s32[]{:T(128)}, bf16[4,1024,128]{2,1,0:T(8,128)(2,1)}, ...), condition=%wide.region_12.13_spmd.clone, body=%wide.region_9.12_spmd.sunk.clone.sunk | while | flops 1998507008 | bytes 75882544 | solution.py:173
  110.4 3.8 %fusion.212 = (f32[1024]{0:T(1024)S(1)}, f32[1024,1024]{0,1:T(8,128)S(1)}) fusion(f32[16,1024]{1,0:T(8,128)S(1)} %dynamic-slice_bitcast_fusion.2, f32[4,16,1024]{2,1,0:T(8,128)S(1)} %get-tuple-element.1167, s32[]{:T(128)S(6)} %copy.77), kind=kOutput, calls=%fused_computation.28.clone.1 | convolution fusion | flops 208665600 | bytes 4329476 | tf_op jit(solution)/shard_map/while/body/eval_jaxpr/dot_general | solution.py:76
  127.4 4.2 %fusion.218 = f32[4,16,1024]{2,1,0:T(8,128)} fusion(f32[4,16,1024]{2,1,0:T(8,128)} %get-tuple-element.1144, s32[]{:T(128)S(6)} %copy.77, f32[16,1024]{1,0:T(8,128)S(1)} %dynamic-slice_bitcast_fusion.2, f32[1024,1024]{0,1:T(8,128)S(1)} %multiply_select_fusion.2), kind=kOutput, calls=%fused_computation.37.clone.1 | convolution fusion | flops 201326592 | bytes 4325380 | tf_op jit(solution)/shard_map/while/body/eval_jaxpr/dot_general | solution.py:97
  134.9 3.8 %fusion.212 = (f32[1024]{0:T(1024)S(1)}, f32[1024,1024]{0,1:T(8,128)S(1)}) fusion(f32[16,1024]{1,0:T(8,128)S(1)} %dynamic-slice_bitcast_fusion.2, f32[4,16,1024]{2,1,0:T(8,128)S(1)} %get-tuple-element.1167, s32[]{:T(128)S(6)} %copy.77), kind=kOutput, calls=%fused_computation.28.clone.1 | convolution fusion | flops 208665600 | bytes 4329476 | tf_op jit(solution)/shard_map/while/body/eval_jaxpr/dot_general | solution.py:76
  149.9 2.1 fusion.217
  152.0 4.2 %fusion.218 = f32[4,16,1024]{2,1,0:T(8,128)} fusion(f32[4,16,1024]{2,1,0:T(8,128)} %get-tuple-element.1144, s32[]{:T(128)S(6)} %copy.77, f32[16,1024]{1,0:T(8,128)S(1)} %dynamic-slice_bitcast_fusion.2, f32[1024,1024]{0,1:T(8,128)S(1)} %multiply_select_fusion.2), kind=kOutput, calls=%fused_computation.37.clone.1 | convolution fusion | flops 201326592 | bytes 4325380 | tf_op jit(solution)/shard_map/while/body/eval_jaxpr/dot_general | solution.py:97
  159.5 3.8 %fusion.212 = (f32[1024]{0:T(1024)S(1)}, f32[1024,1024]{0,1:T(8,128)S(1)}) fusion(f32[16,1024]{1,0:T(8,128)S(1)} %dynamic-slice_bitcast_fusion.2, f32[4,16,1024]{2,1,0:T(8,128)S(1)} %get-tuple-element.1167, s32[]{:T(128)S(6)} %copy.77), kind=kOutput, calls=%fused_computation.28.clone.1 | convolution fusion | flops 208665600 | bytes 4329476 | tf_op jit(solution)/shard_map/while/body/eval_jaxpr/dot_general | solution.py:76
  176.5 4.2 %fusion.218 = f32[4,16,1024]{2,1,0:T(8,128)} fusion(f32[4,16,1024]{2,1,0:T(8,128)} %get-tuple-element.1144, s32[]{:T(128)S(6)} %copy.77, f32[16,1024]{1,0:T(8,128)S(1)} %dynamic-slice_bitcast_fusion.2, f32[1024,1024]{0,1:T(8,128)S(1)} %multiply_select_fusion.2), kind=kOutput, calls=%fused_computation.37.clone.1 | convolution fusion | flops 201326592 | bytes 4325380 | tf_op jit(solution)/shard_map/while/body/eval_jaxpr/dot_general | solution.py:97
  184.0 3.8 %fusion.212 = (f32[1024]{0:T(1024)S(1)}, f32[1024,1024]{0,1:T(8,128)S(1)}) fusion(f32[16,1024]{1,0:T(8,128)S(1)} %dynamic-slice_bitcast_fusion.2, f32[4,16,1024]{2,1,0:T(8,128)S(1)} %get-tuple-element.1167, s32[]{:T(128)S(6)} %copy.77), kind=kOutput, calls=%fused_computation.28.clone.1 | convolution fusion | flops 208665600 | bytes 4329476 | tf_op jit(solution)/shard_map/while/body/eval_jaxpr/dot_general | solution.py:76
  201.0 4.2 %fusion.218 = f32[4,16,1024]{2,1,0:T(8,128)} fusion(f32[4,16,1024]{2,1,0:T(8,128)} %get-tuple-element.1144, s32[]{:T(128)S(6)} %copy.77, f32[16,1024]{1,0:T(8,128)S(1)} %dynamic-slice_bitcast_fusion.2, f32[1024,1024]{0,1:T(8,128)S(1)} %multiply_select_fusion.2), kind=kOutput, calls=%fused_computation.37.clone.1 | convolution fusion | flops 201326592 | bytes 4325380 | tf_op jit(solution)/shard_map/while/body/eval_jaxpr/dot_general | solution.py:97
  207.7 27.9 %all-gather.21.cloned.1.call-done = f32[16,153,128]{2,1,0:T(8,128)} async-done(((f32[4,153,128]{2,1,0:T(8,128)}), f32[16,153,128]{2,1,0:T(8,128)}) %all-gather.21.cloned.1.call-update) | async-done | bytes 1253392 | tf_op jit(solution)/shard_map/all_gather | solution.py:154
  235.6 2.3 fusion.89
  238.0 8.1 %all-gather.10 = f32[4,4,153]{2,1,0:T(4,128)S(1)} all-gather(f32[1,4,153]{2,1,0:T(4,128)S(1)} %bitcast.303), channel_id=8, replica_groups=mesh['seq'=4,'seg'=4,'head'=2] {'seq'}, dimensions={0}, use_global_device_ids=true | all-gather | bytes 12240 | tf_op jit(solution)/shard_map/all_gather | solution.py:155
  246.2 13.7 %all-gather.11 = f32[4,4,153]{2,1,0:T(4,128)S(1)} all-gather(f32[1,4,153]{2,1,0:T(4,128)S(1)} %bitcast.302), channel_id=9, replica_groups=mesh['seq'=4,'seg'=4,'head'=2] {'seg'}, dimensions={0}, use_global_device_ids=true | all-gather | bytes 12240 | tf_op jit(solution)/shard_map/all_gather | solution.py:13
  259.9 10.9 %all-gather.23.cloned.1.call-done = f32[16,153,128]{2,1,0:T(8,128)} async-done(((f32[4,153,128]{2,1,0:T(8,128)}), f32[16,153,128]{2,1,0:T(8,128)}) %all-gather.23.cloned.1.call-update) | async-done | bytes 1253392 | tf_op jit(solution)/shard_map/all_gather | solution.py:13
  272.7 25.7 %while.83 = (s32[]{:T(128)}, f32[4,128,16]{1,2,0:T(8,128)S(1)}, f32[4,128,16]{1,2,0:T(8,128)S(1)}, bf16[4,1024,128]{2,1,0:T(8,128)(2,1)}, bf16[4,16,1024]{2,1,0:...) while((s32[]{:T(128)}, f32[4,128,16]{1,2,0:T(8,128)S(1)}, ...), condition=%wide.region_20.21_spmd.clone, body=%wide.region_19.20_spmd.sunk.clone.sunk | while | flops 156230656 | bytes 5469037 | solution.py:178
  298.4 39.8 %all-reduce = (f32[128,16]{0,1:T(8,128)}, f32[128,16]{0,1:T(8,128)}) all-reduce(f32[128,16]{0,1:T(8,128)S(1)} %reduce_sum.125, f32[128,16]{0,1:T(8,128)S(1)} %reduce_sum.126), channel_id=1, replica_groups=mesh['seq'=4,'seg'=4,'head'=2] {'seq','seg','head'}, use_global_device_ids=true, to_apply=%region_22.23 | all-reduce | flops 4096 | bytes 32768 | tf_op jit(solution)/shard_map/psum | solution.py:182
  (241 shorter events, 127.0 us)
Async XLA Ops:
  7.2 61.0 %all-gather.17.cloned.1.call-start = ((), (), s32[]{:S(2)}) async-start(), calls=%async_computation | async-start | bytes 1638400 | tf_op jit(solution)/shard_map/all_gather | solution.py:154
  35.8 0.7 copy-start.4
  36.6 66.9 %all-gather.19.cloned.1.call-start = ((), (), s32[]{:S(2)}) async-start(), calls=%async_computation.1 | async-start | bytes 1638400 | tf_op jit(solution)/shard_map/all_gather | solution.py:13
  68.1 40.9 %copy-start.2 = (f32[136,16]{1,0:T(8,128)S(1)}, f32[136,16]{1,0:T(8,128)}, u32[]{:S(2)}) copy-start(f32[136,16]{1,0:T(8,128)} %get-tuple-element.1252) | copy-start | bytes 26116
  68.1 40.9 %copy-start.3 = (f32[136,16]{1,0:T(8,128)S(1)}, f32[136,16]{1,0:T(8,128)}, u32[]{:S(2)}) copy-start(f32[136,16]{1,0:T(8,128)} %get-tuple-element.1254) | copy-start | bytes 26116
  68.1 40.9 %copy-start.5 = (f32[136]{0:T(256)S(1)}, f32[136]{0:T(256)}, u32[]{:S(2)}) copy-start(f32[136]{0:T(256)} %get-tuple-element.1271) | copy-start | bytes 1636
  70.5 165.0 %all-gather.21.cloned.1.call-start = ((), (), s32[]{:S(2)}) async-start(), calls=%async_computation.2 | async-start | bytes 1638400 | tf_op jit(solution)/shard_map/all_gather | solution.py:154
  114.3 3.4 copy-start
  119.6 3.9 %copy-start.1 = (f32[1024,1024]{0,1:T(8,128)S(1)}, f32[1024,1024]{0,1:T(8,128)}, u32[]{:S(2)}) copy-start(f32[1024,1024]{0,1:T(8,128)} %copy-done) | copy-start | bytes 12582916 | tf_op jit(solution)/shard_map/while
  123.5 1.9 copy-start.6
  127.4 6.3 %copy-start.7 = (bf16[4,16,1024]{2,1,0:T(8,128)(2,1)}, bf16[4,16,1024]{2,1,0:T(8,128)(2,1)S(1)}, u32[]{:S(2)}) copy-start(bf16[4,16,1024]{2,1,0:T(8,128)(2,1)S(1)} %fusion.217) | copy-start | bytes 393220 | tf_op jit(solution)/shard_map/while
  138.8 3.4 copy-start
  144.1 3.9 %copy-start.1 = (f32[1024,1024]{0,1:T(8,128)S(1)}, f32[1024,1024]{0,1:T(8,128)}, u32[]{:S(2)}) copy-start(f32[1024,1024]{0,1:T(8,128)} %copy-done) | copy-start | bytes 12582916 | tf_op jit(solution)/shard_map/while
  148.0 1.9 copy-start.6
  152.0 6.3 %copy-start.7 = (bf16[4,16,1024]{2,1,0:T(8,128)(2,1)}, bf16[4,16,1024]{2,1,0:T(8,128)(2,1)S(1)}, u32[]{:S(2)}) copy-start(bf16[4,16,1024]{2,1,0:T(8,128)(2,1)S(1)} %fusion.217) | copy-start | bytes 393220 | tf_op jit(solution)/shard_map/while
  163.3 3.4 copy-start
  168.6 3.9 %copy-start.1 = (f32[1024,1024]{0,1:T(8,128)S(1)}, f32[1024,1024]{0,1:T(8,128)}, u32[]{:S(2)}) copy-start(f32[1024,1024]{0,1:T(8,128)} %copy-done) | copy-start | bytes 12582916 | tf_op jit(solution)/shard_map/while
  172.5 1.9 copy-start.6
  176.5 6.3 %copy-start.7 = (bf16[4,16,1024]{2,1,0:T(8,128)(2,1)}, bf16[4,16,1024]{2,1,0:T(8,128)(2,1)S(1)}, u32[]{:S(2)}) copy-start(bf16[4,16,1024]{2,1,0:T(8,128)(2,1)S(1)} %fusion.217) | copy-start | bytes 393220 | tf_op jit(solution)/shard_map/while
  187.8 3.4 copy-start
  193.2 3.9 %copy-start.1 = (f32[1024,1024]{0,1:T(8,128)S(1)}, f32[1024,1024]{0,1:T(8,128)}, u32[]{:S(2)}) copy-start(f32[1024,1024]{0,1:T(8,128)} %copy-done) | copy-start | bytes 12582916 | tf_op jit(solution)/shard_map/while
  197.1 1.9 copy-start.6
  201.0 6.3 %copy-start.7 = (bf16[4,16,1024]{2,1,0:T(8,128)(2,1)}, bf16[4,16,1024]{2,1,0:T(8,128)(2,1)S(1)}, u32[]{:S(2)}) copy-start(bf16[4,16,1024]{2,1,0:T(8,128)(2,1)S(1)} %fusion.217) | copy-start | bytes 393220 | tf_op jit(solution)/shard_map/while
  207.6 63.2 %all-gather.23.cloned.1.call-start = ((), (), s32[]{:S(2)}) async-start(), calls=%async_computation.3 | async-start | bytes 1638400 | tf_op jit(solution)/shard_map/all_gather | solution.py:13
Sparse Core Ops, SparseCore 0:
  36.7 31.3 all-gather.16
  70.7 32.7 all-gather.18
  207.7 27.7 all-gather.20
  238.1 32.7 all-gather.22
where the time goes:
time: 347 us; the launch traced here: 345 us
  matrix products  140 us (40%)
  blocking collectives  83.4 us (24%)
  waiting for transfers between devices  80.6 us (23%)
  between operations  14 us (4%)
  other arithmetic  12.4 us (4%)
  local copies, waits for them, and re-layouts  12.3 us (4%)
    all_gather x2, waiting for transfers between devices, carried(): lax.all_gather(stacked[0], 'seq', axis=0, tiled=True)  59.4 us
    psum x1, blocking collectives, shards(): lax.psum((jnp.sum(grad_q, 0), jnp.sum(grad_k, 0)), ('seq', 'seg', 'head'))  39.8 us
    all_gather x2, blocking collectives, carried_in(): pieces = jax.tree.map(lambda part: lax.all_gather(part, axis), value)  27.4 us
    all_gather x2, waiting for transfers between devices, carried_in(): pieces = jax.tree.map(lambda part: lax.all_gather(part, axis), value)  21.2 us
    dot_general x4, matrix products, head_forward(): g_k = jnp.dot(q_t, g_scores, precision=highest)  16.6 us
    all_gather x2, blocking collectives, carried(): lax.all_gather(stacked[1], 'seq', axis=0, tiled=True)  16.3 us
    dot_general x4, matrix products, head_forward(): lax.dot_general(q_t, k_t, (((0,), (0,)), ((), ())), precision=highest)  15.3 us
    dot_general x8, matrix products, project(): lax.dot_general(weight_b, rows, (((0,), (1,)), ((), ())), preferred_eleme...  9.01 us
  transfers between devices with their start and end apart: 4, of which 4 were waited for; matrix products, arithmetic and copies ran while one was open for 0% of the time, Pallas kernels for 0%

commit v1 on v0

--- a/solution.py
+++ b/solution.py
@@ -6,6 +6,28 @@
 from jax.sharding import PartitionSpec as P
 
 highest = lax.Precision.HIGHEST
+
+
+def in_order(tiles, dim):
+    lengths = list(tiles.shape[1:])
+    lengths[dim] *= tiles.shape[0]
+    return jnp.moveaxis(tiles, 0, dim).reshape(lengths)
+
+
+def gather_around(x, axis, dim):
+    size = lax.axis_size(axis)
+    pairs = [(i, (i + 1) % size) for i in range(size)]
+    back = [(b, a) for a, b in pairs]
+    lower, upper = ([], [])
+    for turn in range(size - 1):
+        if turn % 2 == 0:
+            lower.append(lax.ppermute(lower[-1] if lower else x, axis, pairs))
+        else:
+            upper.append(lax.ppermute(upper[-1] if upper else x, axis, back))
+    blocks = jnp.stack([*lower[::-1], x, *upper])
+    shift = lax.axis_index(axis) - len(lower)
+    blocks = blocks[(jnp.arange(size) - shift) % size]
+    return in_order(blocks, dim)
 
 
 def carried_in(value, axis, join, neutral, backward):
@@ -151,7 +173,7 @@
         backward,
         (zeros, zeros),
         (
-            lax.all_gather(stacked[0], "seq", axis=0, tiled=True),
+            gather_around(stacked[0], "seq", 0),
             lax.all_gather(stacked[1], "seq", axis=0, tiled=True),
         ),
     )

time: 347 us -> 336 us (0.968)
  waiting for transfers between devices: 80.6 us -> 61.6 us
  starting transfers between devices: 0.16 us -> 8.71 us
    all_gather x2 -> x0, waiting for transfers between devices: 59.4 us -> none  [carried(): lax.all_gather(stacked[0], 'seq', axis=0, tiled=True)]
    ppermute x0 -> x6, waiting for transfers between devices: none -> 41.1 us  [the longest x4 28.2 us: gather_around(): lower.append(lax.ppermute(lower[-1] if lower else x, axis, pairs))]
    ppermute x0 -> x6, starting transfers between devices: none -> 8.63 us  [the longest x4 6.13 us: gather_around(): lower.append(lax.ppermute(lower[-1] if lower else x, axis, pairs))]
  transfers between devices with their start and end apart: 4 -> 8, of which waited for: 4 -> 8; matrix products, arithmetic and copies ran while one was open for 0% -> 0% of each run, Pallas kernels for 0% -> 0%
where the time goes in v1:
time: 336 us; the launch traced here: 334 us
  matrix products  140 us (42%)
  blocking collectives  83.6 us (25%)
  waiting for transfers between devices  61.6 us (18%)
  between operations  14.3 us (4%)
  local copies, waits for them, and re-layouts  12.9 us (4%)
  other arithmetic  10.8 us (3%)
  starting transfers between devices  8.71 us (3%)
    psum x1, blocking collectives, shards(): lax.psum((jnp.sum(grad_q, 0), jnp.sum(grad_k, 0)), ('seq', 'seg', 'head'))  39.8 us
    ppermute x4, waiting for transfers between devices, gather_around(): lower.append(lax.ppermute(lower[-1] if lower else x, axis, pairs))  28.2 us
    all_gather x2, blocking collectives, carried_in(): pieces = jax.tree.map(lambda part: lax.all_gather(part, axis), value)  27.4 us
    all_gather x2, waiting for transfers between devices, carried_in(): pieces = jax.tree.map(lambda part: lax.all_gather(part, axis), value)  20.5 us
    dot_general x4, matrix products, head_forward(): g_k = jnp.dot(q_t, g_scores, precision=highest)  16.8 us
    all_gather x2, blocking collectives, carried(): lax.all_gather(stacked[1], 'seq', axis=0, tiled=True)  16.4 us
    dot_general x4, matrix products, head_forward(): lax.dot_general(q_t, k_t, (((0,), (0,)), ((), ())), precision=highest)  15.2 us
    ppermute x2, waiting for transfers between devices, gather_around(): upper.append(lax.ppermute(upper[-1] if upper else x, axis, back))  12.9 us
  transfers between devices with their start and end apart: 8, of which 8 were waited for; matrix products, arithmetic and copies ran while one was open for 0% of the time, Pallas kernels for 0%

profile of v1, /device:TPU:0, one launch (start us, length us, event | category | flops | bytes accessed | tf_op | source)
XLA Modules:
  0.0 333.7 jit_solution(14066489279807718192)
XLA Ops:
  8.7 27.1 %while.81 = (s32[]{:T(128)}, f32[4,16,1024]{2,1,0:T(8,128)S(1)}, f32[4,16,1024]{2,1,0:T(8,128)S(1)}, f32[4,153,128]{2,1,0:T(8,128)S(1)}, f32[4,153]{1,0:T(4,128)...) while((s32[]{:T(128)}, f32[4,16,1024]{2,1,0:T(8,128)S(1)}, ...), condition=%wide.region_2.3_spmd.clone, body=%wide.region_0.2_spmd.sunk.clone.sunk | while | flops 103662440 | bytes 4145861 | solution.py:188
  39.9 8.5 %collective-permute-done = f32[1,4,153,128]{3,2,1,0:T(8,128)S(1)} collective-permute-done((f32[1,4,153,128]{3,2,1,0:T(8,128)S(1)}, f32[1,4,153,128]{3,2,1,0:T(8,128)S(1)}, u32[]{:S(2)}, u32[]{:S(2)}) %collective-permute-start) | collective-permute-done | bytes 313376 | tf_op jit(solution)/shard_map/ppermute | solution.py:24
  49.5 6.5 %collective-permute-done.2 = f32[1,4,153,128]{3,2,1,0:T(8,128)S(1)} collective-permute-done((f32[1,4,153,128]{3,2,1,0:T(8,128)S(1)}, f32[1,4,153,128]{3,2,1,0:T(8,128)S(1)}, u32[]{:S(2)}, u32[]{:S(2)}) %collective-permute-start.2) | collective-permute-done | bytes 313376 | tf_op jit(solution)/shard_map/ppermute | solution.py:26
  55.9 5.6 %collective-permute-done.1 = f32[1,4,153,128]{3,2,1,0:T(8,128)S(1)} collective-permute-done((f32[1,4,153,128]{3,2,1,0:T(8,128)S(1)}, f32[1,4,153,128]{3,2,1,0:T(8,128)S(1)}, u32[]{:S(2)}, u32[]{:S(2)}) %collective-permute-start.1) | collective-permute-done | bytes 313376 | tf_op jit(solution)/shard_map/ppermute | solution.py:24
  63.4 8.4 %all-gather.6 = f32[4,4,153]{2,1,0:T(4,128)S(1)} all-gather(f32[1,4,153]{2,1,0:T(4,128)S(1)} %bitcast.328), channel_id=3, replica_groups=mesh['seq'=4,'seg'=4,'head'=2] {'seq'}, dimensions={0}, use_global_device_ids=true | all-gather | bytes 12240 | tf_op jit(solution)/shard_map/all_gather | solution.py:177
  71.8 13.8 %all-gather.7 = f32[4,4,153]{2,1,0:T(4,128)S(1)} all-gather(f32[1,4,153]{2,1,0:T(4,128)S(1)} %bitcast.325), channel_id=4, replica_groups=mesh['seq'=4,'seg'=4,'head'=2] {'seg'}, dimensions={0}, use_global_device_ids=true | all-gather | bytes 12240 | tf_op jit(solution)/shard_map/all_gather | solution.py:35
  86.3 10.5 %all-gather.13.cloned.1.call-done = f32[16,153,128]{2,1,0:T(8,128)} async-done(((f32[4,153,128]{2,1,0:T(8,128)}), f32[16,153,128]{2,1,0:T(8,128)}) %all-gather.13.cloned.1.call-update) | async-done | bytes 1253392 | tf_op jit(solution)/shard_map/all_gather | solution.py:35
  102.4 98.6 %while.82 = (s32[]{:T(128)}, bf16[4,1024,128]{2,1,0:T(8,128)(2,1)}, bf16[4,16,1024]{2,1,0:T(8,128)(2,1)}, f32[4,16,1024]{2,1,0:T(8,128)}, f32[4,153,128]{2,1,0:T...) while((s32[]{:T(128)}, bf16[4,1024,128]{2,1,0:T(8,128)(2,1)}, ...), condition=%wide.region_12.13_spmd.clone, body=%wide.region_9.12_spmd.sunk.clone.sunk | while | flops 1998507008 | bytes 75882544 | solution.py:195
  103.7 3.8 %fusion.214 = (f32[1024]{0:T(1024)S(1)}, f32[1024,1024]{0,1:T(8,128)S(1)}) fusion(f32[16,1024]{1,0:T(8,128)S(1)} %dynamic-slice_bitcast_fusion.2, f32[4,16,1024]{2,1,0:T(8,128)S(1)} %get-tuple-element.1167, s32[]{:T(128)S(6)} %copy.77), kind=kOutput, calls=%fused_computation.30.clone.1 | convolution fusion | flops 208665600 | bytes 4329476 | tf_op jit(solution)/shard_map/while/body/eval_jaxpr/dot_general | solution.py:98
  120.7 4.2 %fusion.220 = f32[4,16,1024]{2,1,0:T(8,128)} fusion(f32[4,16,1024]{2,1,0:T(8,128)} %get-tuple-element.1144, s32[]{:T(128)S(6)} %copy.77, f32[16,1024]{1,0:T(8,128)S(1)} %dynamic-slice_bitcast_fusion.2, f32[1024,1024]{0,1:T(8,128)S(1)} %multiply_select_fusion.2), kind=kOutput, calls=%fused_computation.39.clone.1 | convolution fusion | flops 201326592 | bytes 4325380 | tf_op jit(solution)/shard_map/while/body/eval_jaxpr/dot_general | solution.py:119
  128.3 3.8 %fusion.214 = (f32[1024]{0:T(1024)S(1)}, f32[1024,1024]{0,1:T(8,128)S(1)}) fusion(f32[16,1024]{1,0:T(8,128)S(1)} %dynamic-slice_bitcast_fusion.2, f32[4,16,1024]{2,1,0:T(8,128)S(1)} %get-tuple-element.1167, s32[]{:T(128)S(6)} %copy.77), kind=kOutput, calls=%fused_computation.30.clone.1 | convolution fusion | flops 208665600 | bytes 4329476 | tf_op jit(solution)/shard_map/while/body/eval_jaxpr/dot_general | solution.py:98
  145.3 4.2 %fusion.220 = f32[4,16,1024]{2,1,0:T(8,128)} fusion(f32[4,16,1024]{2,1,0:T(8,128)} %get-tuple-element.1144, s32[]{:T(128)S(6)} %copy.77, f32[16,1024]{1,0:T(8,128)S(1)} %dynamic-slice_bitcast_fusion.2, f32[1024,1024]{0,1:T(8,128)S(1)} %multiply_select_fusion.2), kind=kOutput, calls=%fused_computation.39.clone.1 | convolution fusion | flops 201326592 | bytes 4325380 | tf_op jit(solution)/shard_map/while/body/eval_jaxpr/dot_general | solution.py:119
  152.8 3.8 %fusion.214 = (f32[1024]{0:T(1024)S(1)}, f32[1024,1024]{0,1:T(8,128)S(1)}) fusion(f32[16,1024]{1,0:T(8,128)S(1)} %dynamic-slice_bitcast_fusion.2, f32[4,16,1024]{2,1,0:T(8,128)S(1)} %get-tuple-element.1167, s32[]{:T(128)S(6)} %copy.77), kind=kOutput, calls=%fused_computation.30.clone.1 | convolution fusion | flops 208665600 | bytes 4329476 | tf_op jit(solution)/shard_map/while/body/eval_jaxpr/dot_general | solution.py:98
  169.8 4.2 %fusion.220 = f32[4,16,1024]{2,1,0:T(8,128)} fusion(f32[4,16,1024]{2,1,0:T(8,128)} %get-tuple-element.1144, s32[]{:T(128)S(6)} %copy.77, f32[16,1024]{1,0:T(8,128)S(1)} %dynamic-slice_bitcast_fusion.2, f32[1024,1024]{0,1:T(8,128)S(1)} %multiply_select_fusion.2), kind=kOutput, calls=%fused_computation.39.clone.1 | convolution fusion | flops 201326592 | bytes 4325380 | tf_op jit(solution)/shard_map/while/body/eval_jaxpr/dot_general | solution.py:119
  177.4 3.8 %fusion.214 = (f32[1024]{0:T(1024)S(1)}, f32[1024,1024]{0,1:T(8,128)S(1)}) fusion(f32[16,1024]{1,0:T(8,128)S(1)} %dynamic-slice_bitcast_fusion.2, f32[4,16,1024]{2,1,0:T(8,128)S(1)} %get-tuple-element.1167, s32[]{:T(128)S(6)} %copy.77), kind=kOutput, calls=%fused_computation.30.clone.1 | convolution fusion | flops 208665600 | bytes 4329476 | tf_op jit(solution)/shard_map/while/body/eval_jaxpr/dot_general | solution.py:98
  194.3 4.2 %fusion.220 = f32[4,16,1024]{2,1,0:T(8,128)} fusion(f32[4,16,1024]{2,1,0:T(8,128)} %get-tuple-element.1144, s32[]{:T(128)S(6)} %copy.77, f32[16,1024]{1,0:T(8,128)S(1)} %dynamic-slice_bitcast_fusion.2, f32[1024,1024]{0,1:T(8,128)S(1)} %multiply_select_fusion.2), kind=kOutput, calls=%fused_computation.39.clone.1 | convolution fusion | flops 201326592 | bytes 4325380 | tf_op jit(solution)/shard_map/while/body/eval_jaxpr/dot_general | solution.py:119
  203.9 8.8 %collective-permute-done.3 = f32[1,4,153,128]{3,2,1,0:T(8,128)S(1)} collective-permute-done((f32[1,4,153,128]{3,2,1,0:T(8,128)}, f32[1,4,153,128]{3,2,1,0:T(8,128)S(1)}, u32[]{:S(2)}, u32[]{:S(2)}) %collective-permute-start.3) | collective-permute-done | bytes 313376 | tf_op jit(solution)/shard_map/ppermute | solution.py:24
  213.2 6.5 %collective-permute-done.5 = f32[1,4,153,128]{3,2,1,0:T(8,128)S(1)} collective-permute-done((f32[1,4,153,128]{3,2,1,0:T(8,128)}, f32[1,4,153,128]{3,2,1,0:T(8,128)S(1)}, u32[]{:S(2)}, u32[]{:S(2)}) %collective-permute-start.5) | collective-permute-done | bytes 313376 | tf_op jit(solution)/shard_map/ppermute | solution.py:26
  219.7 5.3 %collective-permute-done.4 = f32[1,4,153,128]{3,2,1,0:T(8,128)S(1)} collective-permute-done((f32[1,4,153,128]{3,2,1,0:T(8,128)S(1)}, f32[1,4,153,128]{3,2,1,0:T(8,128)S(1)}, u32[]{:S(2)}, u32[]{:S(2)}) %collective-permute-start.4) | collective-permute-done | bytes 313376 | tf_op jit(solution)/shard_map/ppermute | solution.py:24
  227.7 8.1 %all-gather.8 = f32[4,4,153]{2,1,0:T(4,128)S(1)} all-gather(f32[1,4,153]{2,1,0:T(4,128)S(1)} %bitcast.327), channel_id=6, replica_groups=mesh['seq'=4,'seg'=4,'head'=2] {'seq'}, dimensions={0}, use_global_device_ids=true | all-gather | bytes 12240 | tf_op jit(solution)/shard_map/all_gather | solution.py:177
  235.8 13.6 %all-gather.9 = f32[4,4,153]{2,1,0:T(4,128)S(1)} all-gather(f32[1,4,153]{2,1,0:T(4,128)S(1)} %bitcast.326), channel_id=7, replica_groups=mesh['seq'=4,'seg'=4,'head'=2] {'seg'}, dimensions={0}, use_global_device_ids=true | all-gather | bytes 12240 | tf_op jit(solution)/shard_map/all_gather | solution.py:35
  249.5 10.1 %all-gather.15.cloned.1.call-done = f32[16,153,128]{2,1,0:T(8,128)} async-done(((f32[4,153,128]{2,1,0:T(8,128)}), f32[16,153,128]{2,1,0:T(8,128)}) %all-gather.15.cloned.1.call-update) | async-done | bytes 1253392 | tf_op jit(solution)/shard_map/all_gather | solution.py:35
  261.4 25.7 %while.83 = (s32[]{:T(128)}, f32[4,128,16]{1,2,0:T(8,128)S(1)}, f32[4,128,16]{1,2,0:T(8,128)S(1)}, bf16[4,1024,128]{2,1,0:T(8,128)(2,1)}, bf16[4,16,1024]{2,1,0:...) while((s32[]{:T(128)}, f32[4,128,16]{1,2,0:T(8,128)S(1)}, ...), condition=%wide.region_20.21_spmd.clone, body=%wide.region_19.20_spmd.sunk.clone.sunk | while | flops 156230656 | bytes 5469037 | solution.py:200
  287.1 39.8 %all-reduce = (f32[128,16]{0,1:T(8,128)}, f32[128,16]{0,1:T(8,128)}) all-reduce(f32[128,16]{0,1:T(8,128)S(1)} %reduce_sum.125, f32[128,16]{0,1:T(8,128)S(1)} %reduce_sum.126), channel_id=1, replica_groups=mesh['seq'=4,'seg'=4,'head'=2] {'seq','seg','head'}, use_global_device_ids=true, to_apply=%region_22.23 | all-reduce | flops 4096 | bytes 32768 | tf_op jit(solution)/shard_map/psum | solution.py:204
  (251 shorter events, 144.5 us)
Async XLA Ops:
  7.2 89.6 %all-gather.13.cloned.1.call-start = ((), (), s32[]{:S(2)}) async-start(), calls=%async_computation | async-start | bytes 1638400 | tf_op jit(solution)/shard_map/all_gather | solution.py:35
  35.8 12.5 %collective-permute-start = (f32[1,4,153,128]{3,2,1,0:T(8,128)S(1)}, f32[1,4,153,128]{3,2,1,0:T(8,128)S(1)}, u32[]{:S(2)}, u32[]{:S(2)}) collective-permute-start(f32[1,4,153,128]{3,2,1,0:T(8,128)S(1)} %bitcast.310), channel_id=1, source_target_pairs={{0,8},{8,16},{16,24},{24,0},{1,9},{9,17},{17,25},{25,1},{2,10},{10... | collective-permute-start | bytes 940040 | tf_op jit(solution)/shard_map/ppermute | solution.py:24
  38.8 17.1 %collective-permute-start.2 = (f32[1,4,153,128]{3,2,1,0:T(8,128)S(1)}, f32[1,4,153,128]{3,2,1,0:T(8,128)S(1)}, u32[]{:S(2)}, u32[]{:S(2)}) collective-permute-start(f32[1,4,153,128]{3,2,1,0:T(8,128)S(1)} %bitcast.311), channel_id=1, source_target_pairs={{8,0},{16,8},{24,16},{0,24},{9,1},{17,9},{25,17},{1,25},{10,2},{18... | collective-permute-start | bytes 940040 | tf_op jit(solution)/shard_map/ppermute | solution.py:26
  48.3 13.2 %collective-permute-start.1 = (f32[1,4,153,128]{3,2,1,0:T(8,128)S(1)}, f32[1,4,153,128]{3,2,1,0:T(8,128)S(1)}, u32[]{:S(2)}, u32[]{:S(2)}) collective-permute-start(f32[1,4,153,128]{3,2,1,0:T(8,128)S(1)} %collective-permute-done), channel_id=1, source_target_pairs={{0,8},{8,16},{16,24},{24,0},{1,9},{9,17},{17,25},{25,1},{2,10},{10... | collective-permute-start | bytes 940040 | tf_op jit(solution)/shard_map/ppermute | solution.py:24
  62.3 40.1 %copy-start.2 = (f32[136,16]{1,0:T(8,128)S(1)}, f32[136,16]{1,0:T(8,128)}, u32[]{:S(2)}) copy-start(f32[136,16]{1,0:T(8,128)} %get-tuple-element.1250) | copy-start | bytes 26116
  62.3 40.1 %copy-start.3 = (f32[136,16]{1,0:T(8,128)S(1)}, f32[136,16]{1,0:T(8,128)}, u32[]{:S(2)}) copy-start(f32[136,16]{1,0:T(8,128)} %get-tuple-element.1252) | copy-start | bytes 26116
  62.3 40.1 %copy-start.4 = (f32[136]{0:T(256)S(1)}, f32[136]{0:T(256)}, u32[]{:S(2)}) copy-start(f32[136]{0:T(256)} %get-tuple-element.1267) | copy-start | bytes 1636
  63.3 196.2 %all-gather.15.cloned.1.call-start = ((), (), s32[]{:S(2)}) async-start(), calls=%async_computation.1 | async-start | bytes 1638400 | tf_op jit(solution)/shard_map/all_gather | solution.py:35
  107.5 3.4 %copy-start = (f32[1024,1024]{0,1:T(8,128)}, f32[1024,1024]{0,1:T(8,128)S(1)}, u32[]{:S(2)}) copy-start(f32[1024,1024]{0,1:T(8,128)S(1)} %get-tuple-element.1020) | copy-start | bytes 12582916 | tf_op jit(solution)/shard_map/while
  112.9 3.9 %copy-start.1 = (f32[1024,1024]{0,1:T(8,128)S(1)}, f32[1024,1024]{0,1:T(8,128)}, u32[]{:S(2)}) copy-start(f32[1024,1024]{0,1:T(8,128)} %copy-done) | copy-start | bytes 12582916 | tf_op jit(solution)/shard_map/while
  116.8 1.9 copy-start.5
  120.7 6.4 %copy-start.6 = (bf16[4,16,1024]{2,1,0:T(8,128)(2,1)}, bf16[4,16,1024]{2,1,0:T(8,128)(2,1)S(1)}, u32[]{:S(2)}) copy-start(bf16[4,16,1024]{2,1,0:T(8,128)(2,1)S(1)} %fusion.219) | copy-start | bytes 393220 | tf_op jit(solution)/shard_map/while
  132.1 3.4 %copy-start = (f32[1024,1024]{0,1:T(8,128)}, f32[1024,1024]{0,1:T(8,128)S(1)}, u32[]{:S(2)}) copy-start(f32[1024,1024]{0,1:T(8,128)S(1)} %get-tuple-element.1020) | copy-start | bytes 12582916 | tf_op jit(solution)/shard_map/while
  137.4 3.9 %copy-start.1 = (f32[1024,1024]{0,1:T(8,128)S(1)}, f32[1024,1024]{0,1:T(8,128)}, u32[]{:S(2)}) copy-start(f32[1024,1024]{0,1:T(8,128)} %copy-done) | copy-start | bytes 12582916 | tf_op jit(solution)/shard_map/while
  145.3 6.4 %copy-start.6 = (bf16[4,16,1024]{2,1,0:T(8,128)(2,1)}, bf16[4,16,1024]{2,1,0:T(8,128)(2,1)S(1)}, u32[]{:S(2)}) copy-start(bf16[4,16,1024]{2,1,0:T(8,128)(2,1)S(1)} %fusion.219) | copy-start | bytes 393220 | tf_op jit(solution)/shard_map/while
  156.6 3.4 %copy-start = (f32[1024,1024]{0,1:T(8,128)}, f32[1024,1024]{0,1:T(8,128)S(1)}, u32[]{:S(2)}) copy-start(f32[1024,1024]{0,1:T(8,128)S(1)} %get-tuple-element.1020) | copy-start | bytes 12582916 | tf_op jit(solution)/shard_map/while
  161.9 3.9 %copy-start.1 = (f32[1024,1024]{0,1:T(8,128)S(1)}, f32[1024,1024]{0,1:T(8,128)}, u32[]{:S(2)}) copy-start(f32[1024,1024]{0,1:T(8,128)} %copy-done) | copy-start | bytes 12582916 | tf_op jit(solution)/shard_map/while
  169.8 6.4 %copy-start.6 = (bf16[4,16,1024]{2,1,0:T(8,128)(2,1)}, bf16[4,16,1024]{2,1,0:T(8,128)(2,1)S(1)}, u32[]{:S(2)}) copy-start(bf16[4,16,1024]{2,1,0:T(8,128)(2,1)S(1)} %fusion.219) | copy-start | bytes 393220 | tf_op jit(solution)/shard_map/while
  181.2 3.4 %copy-start = (f32[1024,1024]{0,1:T(8,128)}, f32[1024,1024]{0,1:T(8,128)S(1)}, u32[]{:S(2)}) copy-start(f32[1024,1024]{0,1:T(8,128)S(1)} %get-tuple-element.1020) | copy-start | bytes 12582916 | tf_op jit(solution)/shard_map/while
  186.5 3.9 %copy-start.1 = (f32[1024,1024]{0,1:T(8,128)S(1)}, f32[1024,1024]{0,1:T(8,128)}, u32[]{:S(2)}) copy-start(f32[1024,1024]{0,1:T(8,128)} %copy-done) | copy-start | bytes 12582916 | tf_op jit(solution)/shard_map/while
  194.3 6.4 %copy-start.6 = (bf16[4,16,1024]{2,1,0:T(8,128)(2,1)}, bf16[4,16,1024]{2,1,0:T(8,128)(2,1)S(1)}, u32[]{:S(2)}) copy-start(bf16[4,16,1024]{2,1,0:T(8,128)(2,1)S(1)} %fusion.219) | copy-start | bytes 393220 | tf_op jit(solution)/shard_map/while
  200.9 11.7 %collective-permute-start.3 = (f32[1,4,153,128]{3,2,1,0:T(8,128)}, f32[1,4,153,128]{3,2,1,0:T(8,128)S(1)}, u32[]{:S(2)}, u32[]{:S(2)}) collective-permute-start(f32[1,4,153,128]{3,2,1,0:T(8,128)} %bitcast.307), channel_id=1, source_target_pairs={{0,8},{8,16},{16,24},{24,0},{1,9},{9,17},{17,25},{25,1},{2,10},{10... | collective-permute-start | bytes 940040 | tf_op jit(solution)/shard_map/ppermute | solution.py:24
  202.4 17.3 %collective-permute-start.5 = (f32[1,4,153,128]{3,2,1,0:T(8,128)}, f32[1,4,153,128]{3,2,1,0:T(8,128)S(1)}, u32[]{:S(2)}, u32[]{:S(2)}) collective-permute-start(f32[1,4,153,128]{3,2,1,0:T(8,128)} %bitcast.308), channel_id=1, source_target_pairs={{8,0},{16,8},{24,16},{0,24},{9,1},{17,9},{25,17},{1,25},{10,2},{18... | collective-permute-start | bytes 940040 | tf_op jit(solution)/shard_map/ppermute | solution.py:26
  212.7 12.3 %collective-permute-start.4 = (f32[1,4,153,128]{3,2,1,0:T(8,128)S(1)}, f32[1,4,153,128]{3,2,1,0:T(8,128)S(1)}, u32[]{:S(2)}, u32[]{:S(2)}) collective-permute-start(f32[1,4,153,128]{3,2,1,0:T(8,128)S(1)} %collective-permute-done.3), channel_id=1, source_target_pairs={{0,8},{8,16},{16,24},{24,0},{1,9},{9,17},{17,25},{25,1},{2,10},{10... | collective-permute-start | bytes 940040 | tf_op jit(solution)/shard_map/ppermute | solution.py:24
  (3 other events, 5.6 us)
Sparse Core Ops, SparseCore 0:
  63.4 33.2 all-gather.12
  227.8 31.7 all-gather.14
